TPU v7x, 8 devices: a whole 2x2x1 slice. The times are simulated.
8 devices in a mesh: dp: 2 (over z, y), sp: 4 (over x, core).
Axes of the slice: x: 2, y: 2, z: 1, core: 2. Of those that a mesh axis runs over, the one named last changes fastest.
Arguments:
- hidden: bfloat16 [32, 2048, 1024], P('dp', 'sp'), parts along dimension 0
- positions: int32 [32, 2048], P('dp', 'sp'), parts along dimension 0
- norm_attn: float32 [4, 1024], replicated
- norm_mlp: float32 [4, 1024], replicated
- w_query: bfloat16 [4, 1024, 16, 64], replicated
- w_key: bfloat16 [4, 1024, 16, 64], replicated
- w_value: bfloat16 [4, 1024, 16, 64], replicated
- w_out: bfloat16 [4, 16, 64, 1024], replicated
- w_gate: bfloat16 [4, 1024, 4096], replicated
- w_up: bfloat16 [4, 1024, 4096], replicated
- w_down: bfloat16 [4, 4096, 1024], replicated
Outputs:
- output: bfloat16 [32, 2048, 1024], P('dp', 'sp'), parts along dimension 0
There are 2 independent parts. A program takes and returns all parts, laid end to end along the dimension named above; an argument that names none is the same for every part.
All inputs are finite; a program needn't handle non-finite values.
Results may differ from a plain program's by a relative error of at most 0.02.
Values are sent between devices in bfloat16 or wider.
A program may use at most 1 GiB of HBM per device.

v0:
```python
import math
import jax
import jax.numpy as jnp
from jax import lax
from jax.sharding import PartitionSpec as P

WINDOW = 512
QUERY_BLOCK = 256
EPS = 1e-5
ROPE_THETA = 10000.0


def rms_norm(hidden, gain):
    x_f32 = hidden.astype(jnp.float32)
    inv_rms = lax.rsqrt(jnp.mean(x_f32 * x_f32, axis=-1, keepdims=True) + EPS)
    return (x_f32 * inv_rms * gain).astype(jnp.bfloat16)


def rotate(vectors, cos_a, sin_a):
    half = vectors.shape[-1] // 2
    first = vectors[..., :half]
    second = vectors[..., half:]
    return jnp.concatenate([first * cos_a - second * sin_a, second * cos_a + first * sin_a], axis=-1)


def rope_tables(positions, head_dim):
    half = head_dim // 2
    inv_freq = ROPE_THETA ** (-2.0 * jnp.arange(half, dtype=jnp.float32) / head_dim)
    angle = positions.astype(jnp.float32)[..., None, None] * inv_freq
    return jnp.cos(angle), jnp.sin(angle)


def project_qkv(hidden, gain, w_query, w_key, w_value, cos_a, sin_a):
    batch, tokens, model_dim = hidden.shape
    heads, head_dim = w_query.shape[1], w_query.shape[2]
    kv_heads = w_key.shape[1]
    normed = rms_norm(hidden, gain)
    query = jnp.dot(normed, w_query.reshape(model_dim, heads * head_dim), preferred_element_type=jnp.float32)
    key_r = jnp.dot(normed, w_key.reshape(model_dim, kv_heads * head_dim), preferred_element_type=jnp.float32)
    value_r = jnp.dot(normed, w_value.reshape(model_dim, kv_heads * head_dim), preferred_element_type=jnp.float32)
    query = rotate(query.reshape(batch, tokens, heads, head_dim), cos_a, sin_a).astype(jnp.bfloat16)
    key_r = rotate(key_r.reshape(batch, tokens, kv_heads, head_dim), cos_a, sin_a).astype(jnp.bfloat16)
    value_r = value_r.astype(jnp.bfloat16).reshape(batch, tokens, kv_heads, head_dim)
    return query.reshape(batch, tokens, kv_heads, heads // kv_heads, head_dim), key_r, value_r


def feed_forward(mixed, gain, w_gate, w_up, w_down):
    normed = rms_norm(mixed, gain)
    gate = jnp.dot(normed, w_gate, preferred_element_type=jnp.float32).astype(jnp.bfloat16)
    up_proj = jnp.dot(normed, w_up, preferred_element_type=jnp.float32).astype(jnp.bfloat16)
    hidden_act = (jax.nn.silu(gate.astype(jnp.float32)) * up_proj.astype(jnp.float32)).astype(jnp.bfloat16)
    return (mixed.astype(jnp.float32) + jnp.dot(hidden_act, w_down, preferred_element_type=jnp.float32)).astype(jnp.bfloat16)


def window_attention(query, key_ext, value_ext, first_key):
    batch, tokens = query.shape[0], query.shape[1]
    span = QUERY_BLOCK + WINDOW - 1
    scale = 1.0 / math.sqrt(query.shape[-1])
    rows = jnp.arange(QUERY_BLOCK)[:, None]
    cols = jnp.arange(span)[None, :]
    band = (cols >= rows) & (cols <= rows + WINDOW - 1)

    def one_block(block_idx):
        start = block_idx * QUERY_BLOCK
        query_blk = lax.dynamic_slice_in_dim(query, start, QUERY_BLOCK, axis=1)
        key_blk = lax.dynamic_slice_in_dim(key_ext, start, span, axis=1)
        value_blk = lax.dynamic_slice_in_dim(value_ext, start, span, axis=1)
        scores = jnp.einsum('bqhgd,bkhd->bhgqk', query_blk, key_blk, preferred_element_type=jnp.float32) * scale
        valid = band & (first_key + start + cols >= 0)
        scores = jnp.where(valid, scores, -1e30)
        probabilities = jax.nn.softmax(scores, axis=-1).astype(jnp.bfloat16)
        return jnp.einsum('bhgqk,bkhd->bqhgd', probabilities, value_blk, preferred_element_type=jnp.float32).astype(jnp.bfloat16)

    blocks = lax.map(one_block, jnp.arange(tokens // QUERY_BLOCK))
    return jnp.moveaxis(blocks, 0, 1).reshape(batch, tokens, -1)


def solution(mesh):
    seq_devices = mesh.shape['sp']
    neighbours = [(source_idx, source_idx + 1) for source_idx in range(seq_devices - 1)]

    def local_stack(hidden, positions, norm_attn, norm_mlp, w_query, w_key, w_value, w_out, w_gate, w_up, w_down):
        batch, tokens, model_dim = hidden.shape
        layers, heads, head_dim = w_query.shape[0], w_query.shape[2], w_query.shape[3]
        halo = WINDOW - 1
        first_key = lax.axis_index('sp') * tokens - halo
        cos_a, sin_a = rope_tables(positions, head_dim)
        for layer in range(layers):
            query, key_r, value_r = project_qkv(hidden, norm_attn[layer], w_query[layer], w_key[layer], w_value[layer], cos_a, sin_a)
            key_halo, value_halo = lax.ppermute((key_r[:, tokens - halo:], value_r[:, tokens - halo:]), 'sp', neighbours)
            key_ext = jnp.concatenate([key_halo, key_r], axis=1)
            value_ext = jnp.concatenate([value_halo, value_r], axis=1)
            attended = window_attention(query, key_ext, value_ext, first_key)
            mixed = (hidden.astype(jnp.float32) + jnp.dot(attended, w_out[layer].reshape(heads * head_dim, model_dim), preferred_element_type=jnp.float32)).astype(jnp.bfloat16)
            hidden = feed_forward(mixed, norm_mlp[layer], w_gate[layer], w_up[layer], w_down[layer])
        return hidden

    row_spec = P('dp', 'sp', None)
    return jax.shard_map(local_stack, mesh=mesh,
                         in_specs=(row_spec, P('dp', 'sp'), P(), P(), P(), P(), P(), P(), P(), P(), P()),
                         out_specs=row_spec, check_vma=False)
```

profile of v0, /device:TPU:1, one launch (start us, length us, event | category | flops | bytes accessed | tf_op | source)
XLA Modules:
  0.0 5210.4 jit_solution(10800825175533248304)
XLA Ops:
  209.1 91.1 %collective-permute-done.1 = bf16[16,511,16,64]{1,3,2,0:T(8,128)(2,1)} collective-permute-done((bf16[16,511,16,64]{1,3,2,0:T(8,128)(2,1)}, bf16[16,511,16,64]{1,3,2,0:T(8,128)(2,1)}, u32[]{:S(2)}, u32[]{:S(2)}) %collective-permute-start.1) | collective-permute-done | bytes 16744480 | tf_op jit(solution)/shard_map/ppermute | solution.py:90
  324.0 156.0 %collective-permute-done = bf16[16,511,16,64]{1,3,2,0:T(8,128)(2,1)} collective-permute-done((bf16[16,511,16,64]{1,3,2,0:T(8,128)(2,1)}, bf16[16,511,16,64]{1,3,2,0:T(8,128)(2,1)}, u32[]{:S(2)}, u32[]{:S(2)}) %collective-permute-start) | collective-permute-done | bytes 16744480 | tf_op jit(solution)/shard_map/ppermute | solution.py:90
  509.7 455.5 %while.44 = (s32[]{:T(128)}, bf16[2,16,256,16,1,64]{2,5,3,1,4,0:T(8,128)(2,1)}, s32[2]{0:T(128)}, bf16[16,1023,16,64]{1,3,2,0:T(8,128)(2,1)}, s32[]{:T(128)}, /*...) while((s32[]{:T(128)}, ...), condition=%wide.region_4.5_spmd.clone, body=%wide.region_1.4_spmd.clone.sunk | while | flops 13476167680 | bytes 672663808 | solution.py:74
  512.7 85.5 %fusion.413 = (f32[16,16,256]{2,1,0:T(8,128)S(1)}, f32[16,16,767,256]{3,2,1,0:T(8,128)}) fusion(pred[256,767]{0,1:T(8,128)(4,1)S(1)} %fusion.412, bf16[16,512,16,1,64]{1,4,2,0,3:T(8,128)(2,1)} %get-tuple-element.649, s32[]{:T(128)S(6)} %select_n.127, bf16[16,1023,16,64]{1,3,2,0:T(8,128)(2,1)} %get-tuple-element.648, s32[]{:T(128)S(6)} %select_n.128), kind=kOutput, calls=%fused_computation.12.clone.3 | convolution fusion | flops 6584795136 | bytes 235077376 | tf_op jit(solution)/shard_map/while/body/eval_jaxpr/bqhgd,bkhd->bhgqk/dot_general | solution.py:68
  598.2 60.9 %fusion.414 = f32[16,16,256]{2,1,0:T(8,128)S(1)} fusion(f32[16,16,767,256]{3,2,1,0:T(8,128)} %get-tuple-element.585, f32[16,16,256]{2,1,0:T(8,128)S(1)} %get-tuple-element.586, pred[256,767]{0,1:T(8,128)(4,1)S(1)} %fusion.412), kind=kLoop, calls=%fused_computation.11.clone.1 | loop fusion | flops 200998912 | bytes 201785088 | tf_op jit(solution)/shard_map/while/body/eval_jaxpr/reduce_sum | solution.py:71
  659.2 79.6 %bitcast_dynamic-update-slice_fusion.8 = bf16[2,16,256,16,1,64]{2,5,3,1,4,0:T(8,128)(2,1)} fusion(bf16[2,16,256,16,1,64]{2,5,3,1,4,0:T(8,128)(2,1)} %get-tuple-element.631, s32[]{:T(128)} %get-tuple-element.630, f32[16,16,256]{2,1,0:T(8,128)S(1)} %fusion.414, f32[16,16,256]{2,1,0:T(8,128)S(1)} %get-tuple-element.586, ...), kind=kOutput, calls=%fused_computation.18.clone.2 | convolution fusion | flops 6689587200 | bytes 235602176 | tf_op jit(solution)/shard_map/while/body/eval_jaxpr/bhgqk,bkhd->bqhgd/dot_general | solution.py:72
  741.6 84.0 %fusion.413 = (f32[16,16,256]{2,1,0:T(8,128)S(1)}, f32[16,16,767,256]{3,2,1,0:T(8,128)}) fusion(pred[256,767]{0,1:T(8,128)(4,1)S(1)} %fusion.412, bf16[16,512,16,1,64]{1,4,2,0,3:T(8,128)(2,1)} %get-tuple-element.649, s32[]{:T(128)S(6)} %select_n.127, bf16[16,1023,16,64]{1,3,2,0:T(8,128)(2,1)} %get-tuple-element.648, s32[]{:T(128)S(6)} %select_n.128), kind=kOutput, calls=%fused_computation.12.clone.3 | convolution fusion | flops 6584795136 | bytes 235077376 | tf_op jit(solution)/shard_map/while/body/eval_jaxpr/bqhgd,bkhd->bhgqk/dot_general | solution.py:68
  825.6 60.9 %fusion.414 = f32[16,16,256]{2,1,0:T(8,128)S(1)} fusion(f32[16,16,767,256]{3,2,1,0:T(8,128)} %get-tuple-element.585, f32[16,16,256]{2,1,0:T(8,128)S(1)} %get-tuple-element.586, pred[256,767]{0,1:T(8,128)(4,1)S(1)} %fusion.412), kind=kLoop, calls=%fused_computation.11.clone.1 | loop fusion | flops 200998912 | bytes 201785088 | tf_op jit(solution)/shard_map/while/body/eval_jaxpr/reduce_sum | solution.py:71
  886.6 78.7 %bitcast_dynamic-update-slice_fusion.8 = bf16[2,16,256,16,1,64]{2,5,3,1,4,0:T(8,128)(2,1)} fusion(bf16[2,16,256,16,1,64]{2,5,3,1,4,0:T(8,128)(2,1)} %get-tuple-element.631, s32[]{:T(128)} %get-tuple-element.630, f32[16,16,256]{2,1,0:T(8,128)S(1)} %fusion.414, f32[16,16,256]{2,1,0:T(8,128)S(1)} %get-tuple-element.586, ...), kind=kOutput, calls=%fused_computation.18.clone.2 | convolution fusion | flops 6689587200 | bytes 235602176 | tf_op jit(solution)/shard_map/while/body/eval_jaxpr/bhgqk,bkhd->bqhgd/dot_general | solution.py:72
  1056.9 78.5 %fusion.188 = bf16[16,512,4096]{2,1,0:T(8,128)(2,1)} fusion(bf16[16,512,1024]{2,1,0:T(8,128)(2,1)} %get-tuple-element.392, f32[1024]{0:T(1024)S(1)} %bitcast.527, f32[16,512]{1,0:T(8,128)S(1)} %add_rsqrt_fusion.6, bf16[4,1024,4096]{2,1,0:T(8,128)(2,1)} %param.28), kind=kOutput, calls=%fused_computation.242 | convolution fusion | flops 68753031168 | bytes 92311552 | tf_op jit(solution)/shard_map/dot_general | solution.py:50
  1135.4 97.2 %fusion.175.clone.5 = bf16[16,512,4096]{2,1,0:T(8,128)(2,1)} fusion(bf16[16,512,4096]{2,1,0:T(8,128)(2,1)} %fusion.188, bf16[16,512,1024]{2,1,0:T(8,128)(2,1)} %get-tuple-element.392, f32[1024]{0:T(1024)S(1)} %bitcast.528, f32[16,512]{1,0:T(8,128)S(1)} %add_rsqrt_fusion.6, bf16[4,1024,4096]{2,1,0:T(8,128)(2,1)} %param.27), kind=kOutput, calls=%fused_computation.127.clone.clone.clone.clone.clone.clone.2 | convolution fusion | flops 69055021056 | bytes 159420416 | tf_op jit(solution)/shard_map/dot_general | solution.py:49
  1232.6 79.7 %fusion.128 = (f32[16,512]{1,0:T(8,128)S(1)}, bf16[16,512,1024]{2,1,0:T(8,128)(2,1)}) fusion(bf16[4,4096,1024]{2,1,0:T(8,128)(2,1)} %param.29, bf16[16,512,1024]{2,1,0:T(8,128)(2,1)} %get-tuple-element.392, bf16[16,512,4096]{2,1,0:T(8,128)(2,1)} %fusion.175.clone.5), kind=kOutput, calls=%fused_computation.164 | convolution fusion | flops 68769800192 | bytes 109084672 | tf_op jit(solution)/shard_map/dot_general | solution.py:52
  1499.3 100.8 %collective-permute-done.3 = bf16[16,511,16,64]{1,3,2,0:T(8,128)(2,1)} collective-permute-done((bf16[16,511,16,64]{1,3,2,0:T(8,128)(2,1)}, bf16[16,511,16,64]{1,3,2,0:T(8,128)(2,1)}, u32[]{:S(2)}, u32[]{:S(2)}) %collective-permute-start.3) | collective-permute-done | bytes 16744480 | tf_op jit(solution)/shard_map/ppermute | solution.py:90
  1623.8 156.0 %collective-permute-done.2 = bf16[16,511,16,64]{1,3,2,0:T(8,128)(2,1)} collective-permute-done((bf16[16,511,16,64]{1,3,2,0:T(8,128)(2,1)}, bf16[16,511,16,64]{1,3,2,0:T(8,128)(2,1)}, u32[]{:S(2)}, u32[]{:S(2)}) %collective-permute-start.2) | collective-permute-done | bytes 16744480 | tf_op jit(solution)/shard_map/ppermute | solution.py:90
  1809.5 455.6 %while.45 = (s32[]{:T(128)}, bf16[2,16,256,16,1,64]{2,5,3,1,4,0:T(8,128)(2,1)}, s32[2]{0:T(128)}, bf16[16,1023,16,64]{1,3,2,0:T(8,128)(2,1)}, s32[]{:T(128)}, /*...) while((s32[]{:T(128)}, ...), condition=%wide.region_10.11_spmd.clone, body=%wide.region_7.10_spmd.clone.sunk | while | flops 13476167680 | bytes 672663808 | solution.py:74
  1812.5 85.6 %fusion.418 = (f32[16,16,256]{2,1,0:T(8,128)S(1)}, f32[16,16,767,256]{3,2,1,0:T(8,128)}) fusion(pred[256,767]{0,1:T(8,128)(4,1)S(1)} %fusion.417, bf16[16,512,16,1,64]{1,4,2,0,3:T(8,128)(2,1)} %get-tuple-element.688, s32[]{:T(128)S(6)} %select_n.132, bf16[16,1023,16,64]{1,3,2,0:T(8,128)(2,1)} %get-tuple-element.687, s32[]{:T(128)S(6)} %select_n.133), kind=kOutput, calls=%fused_computation.35.clone.1 | convolution fusion | flops 6584795136 | bytes 235077376 | tf_op jit(solution)/shard_map/while/body/eval_jaxpr/bqhgd,bkhd->bhgqk/dot_general | solution.py:68
  1898.0 60.9 %fusion.419 = f32[16,16,256]{2,1,0:T(8,128)S(1)} fusion(f32[16,16,767,256]{3,2,1,0:T(8,128)} %get-tuple-element.595, f32[16,16,256]{2,1,0:T(8,128)S(1)} %get-tuple-element.596, pred[256,767]{0,1:T(8,128)(4,1)S(1)} %fusion.417), kind=kLoop, calls=%fused_computation.34.clone.1 | loop fusion | flops 200998912 | bytes 201785088 | tf_op jit(solution)/shard_map/while/body/eval_jaxpr/reduce_sum | solution.py:71
  1959.0 79.6 %bitcast_dynamic-update-slice_fusion.9 = bf16[2,16,256,16,1,64]{2,5,3,1,4,0:T(8,128)(2,1)} fusion(bf16[2,16,256,16,1,64]{2,5,3,1,4,0:T(8,128)(2,1)} %get-tuple-element.670, s32[]{:T(128)} %get-tuple-element.669, f32[16,16,256]{2,1,0:T(8,128)S(1)} %fusion.419, f32[16,16,256]{2,1,0:T(8,128)S(1)} %get-tuple-element.596, ...), kind=kOutput, calls=%fused_computation.41.clone.1 | convolution fusion | flops 6689587200 | bytes 235602176 | tf_op jit(solution)/shard_map/while/body/eval_jaxpr/bhgqk,bkhd->bqhgd/dot_general | solution.py:72
  2041.4 84.0 %fusion.418 = (f32[16,16,256]{2,1,0:T(8,128)S(1)}, f32[16,16,767,256]{3,2,1,0:T(8,128)}) fusion(pred[256,767]{0,1:T(8,128)(4,1)S(1)} %fusion.417, bf16[16,512,16,1,64]{1,4,2,0,3:T(8,128)(2,1)} %get-tuple-element.688, s32[]{:T(128)S(6)} %select_n.132, bf16[16,1023,16,64]{1,3,2,0:T(8,128)(2,1)} %get-tuple-element.687, s32[]{:T(128)S(6)} %select_n.133), kind=kOutput, calls=%fused_computation.35.clone.1 | convolution fusion | flops 6584795136 | bytes 235077376 | tf_op jit(solution)/shard_map/while/body/eval_jaxpr/bqhgd,bkhd->bhgqk/dot_general | solution.py:68
  2125.5 60.9 %fusion.419 = f32[16,16,256]{2,1,0:T(8,128)S(1)} fusion(f32[16,16,767,256]{3,2,1,0:T(8,128)} %get-tuple-element.595, f32[16,16,256]{2,1,0:T(8,128)S(1)} %get-tuple-element.596, pred[256,767]{0,1:T(8,128)(4,1)S(1)} %fusion.417), kind=kLoop, calls=%fused_computation.34.clone.1 | loop fusion | flops 200998912 | bytes 201785088 | tf_op jit(solution)/shard_map/while/body/eval_jaxpr/reduce_sum | solution.py:71
  2186.4 78.7 %bitcast_dynamic-update-slice_fusion.9 = bf16[2,16,256,16,1,64]{2,5,3,1,4,0:T(8,128)(2,1)} fusion(bf16[2,16,256,16,1,64]{2,5,3,1,4,0:T(8,128)(2,1)} %get-tuple-element.670, s32[]{:T(128)} %get-tuple-element.669, f32[16,16,256]{2,1,0:T(8,128)S(1)} %fusion.419, f32[16,16,256]{2,1,0:T(8,128)S(1)} %get-tuple-element.596, ...), kind=kOutput, calls=%fused_computation.41.clone.1 | convolution fusion | flops 6689587200 | bytes 235602176 | tf_op jit(solution)/shard_map/while/body/eval_jaxpr/bhgqk,bkhd->bqhgd/dot_general | solution.py:72
  2356.7 78.5 %fusion.184 = bf16[16,512,4096]{2,1,0:T(8,128)(2,1)} fusion(bf16[16,512,1024]{2,1,0:T(8,128)(2,1)} %get-tuple-element.396, f32[1024]{0:T(1024)S(1)} %bitcast.522, f32[16,512]{1,0:T(8,128)S(1)} %add_rsqrt_fusion.4, bf16[4,1024,4096]{2,1,0:T(8,128)(2,1)} %param.28), kind=kOutput, calls=%fused_computation.240 | convolution fusion | flops 68753031168 | bytes 92311552 | tf_op jit(solution)/shard_map/dot_general | solution.py:50
  2435.2 97.2 %fusion.173.clone.5 = bf16[16,512,4096]{2,1,0:T(8,128)(2,1)} fusion(bf16[16,512,4096]{2,1,0:T(8,128)(2,1)} %fusion.184, bf16[16,512,1024]{2,1,0:T(8,128)(2,1)} %get-tuple-element.396, f32[1024]{0:T(1024)S(1)} %bitcast.523, f32[16,512]{1,0:T(8,128)S(1)} %add_rsqrt_fusion.4, bf16[4,1024,4096]{2,1,0:T(8,128)(2,1)} %param.27), kind=kOutput, calls=%fused_computation.126.clone.clone.clone.clone.clone.clone.2 | convolution fusion | flops 69055021056 | bytes 159420416 | tf_op jit(solution)/shard_map/dot_general | solution.py:49
  2532.4 79.7 %fusion.136 = (f32[16,512]{1,0:T(8,128)S(1)}, bf16[16,512,1024]{2,1,0:T(8,128)(2,1)}) fusion(bf16[4,4096,1024]{2,1,0:T(8,128)(2,1)} %param.29, bf16[16,512,1024]{2,1,0:T(8,128)(2,1)} %get-tuple-element.396, bf16[16,512,4096]{2,1,0:T(8,128)(2,1)} %fusion.173.clone.5), kind=kOutput, calls=%fused_computation.172 | convolution fusion | flops 68769800192 | bytes 109084672 | tf_op jit(solution)/shard_map/dot_general | solution.py:52
  2799.1 100.8 %collective-permute-done.5 = bf16[16,511,16,64]{1,3,2,0:T(8,128)(2,1)} collective-permute-done((bf16[16,511,16,64]{1,3,2,0:T(8,128)(2,1)}, bf16[16,511,16,64]{1,3,2,0:T(8,128)(2,1)}, u32[]{:S(2)}, u32[]{:S(2)}) %collective-permute-start.5) | collective-permute-done | bytes 16744480 | tf_op jit(solution)/shard_map/ppermute | solution.py:90
  2923.6 156.0 %collective-permute-done.4 = bf16[16,511,16,64]{1,3,2,0:T(8,128)(2,1)} collective-permute-done((bf16[16,511,16,64]{1,3,2,0:T(8,128)(2,1)}, bf16[16,511,16,64]{1,3,2,0:T(8,128)(2,1)}, u32[]{:S(2)}, u32[]{:S(2)}) %collective-permute-start.4) | collective-permute-done | bytes 16744480 | tf_op jit(solution)/shard_map/ppermute | solution.py:90
  3109.3 455.4 %while.46 = (s32[]{:T(128)}, bf16[2,16,256,16,1,64]{2,5,3,1,4,0:T(8,128)(2,1)}, s32[2]{0:T(128)}, bf16[16,1023,16,64]{1,3,2,0:T(8,128)(2,1)}, s32[]{:T(128)}, /*...) while((s32[]{:T(128)}, ...), condition=%wide.region_16.17_spmd.clone, body=%wide.region_13.16_spmd.clone.sunk | while | flops 13476167680 | bytes 672663808 | solution.py:74
  3112.2 85.6 %fusion.423 = (f32[16,16,256]{2,1,0:T(8,128)S(1)}, f32[16,16,767,256]{3,2,1,0:T(8,128)}) fusion(pred[256,767]{0,1:T(8,128)(4,1)S(1)} %fusion.422, bf16[16,512,16,1,64]{1,4,2,0,3:T(8,128)(2,1)} %get-tuple-element.727, s32[]{:T(128)S(6)} %select_n.137, bf16[16,1023,16,64]{1,3,2,0:T(8,128)(2,1)} %get-tuple-element.726, s32[]{:T(128)S(6)} %select_n.138), kind=kOutput, calls=%fused_computation.58.clone.1 | convolution fusion | flops 6584795136 | bytes 235077376 | tf_op jit(solution)/shard_map/while/body/eval_jaxpr/bqhgd,bkhd->bhgqk/dot_general | solution.py:68
  3197.8 60.9 %fusion.424 = f32[16,16,256]{2,1,0:T(8,128)S(1)} fusion(f32[16,16,767,256]{3,2,1,0:T(8,128)} %get-tuple-element.605, f32[16,16,256]{2,1,0:T(8,128)S(1)} %get-tuple-element.606, pred[256,767]{0,1:T(8,128)(4,1)S(1)} %fusion.422), kind=kLoop, calls=%fused_computation.57.clone.1 | loop fusion | flops 200998912 | bytes 201785088 | tf_op jit(solution)/shard_map/while/body/eval_jaxpr/reduce_sum | solution.py:71
  3258.7 79.6 %bitcast_dynamic-update-slice_fusion.10 = bf16[2,16,256,16,1,64]{2,5,3,1,4,0:T(8,128)(2,1)} fusion(bf16[2,16,256,16,1,64]{2,5,3,1,4,0:T(8,128)(2,1)} %get-tuple-element.709, s32[]{:T(128)} %get-tuple-element.708, f32[16,16,256]{2,1,0:T(8,128)S(1)} %fusion.424, f32[16,16,256]{2,1,0:T(8,128)S(1)} %get-tuple-element.606, ...), kind=kOutput, calls=%fused_computation.64.clone.1 | convolution fusion | flops 6689587200 | bytes 235602176 | tf_op jit(solution)/shard_map/while/body/eval_jaxpr/bhgqk,bkhd->bqhgd/dot_general | solution.py:72
  3341.1 84.0 %fusion.423 = (f32[16,16,256]{2,1,0:T(8,128)S(1)}, f32[16,16,767,256]{3,2,1,0:T(8,128)}) fusion(pred[256,767]{0,1:T(8,128)(4,1)S(1)} %fusion.422, bf16[16,512,16,1,64]{1,4,2,0,3:T(8,128)(2,1)} %get-tuple-element.727, s32[]{:T(128)S(6)} %select_n.137, bf16[16,1023,16,64]{1,3,2,0:T(8,128)(2,1)} %get-tuple-element.726, s32[]{:T(128)S(6)} %select_n.138), kind=kOutput, calls=%fused_computation.58.clone.1 | convolution fusion | flops 6584795136 | bytes 235077376 | tf_op jit(solution)/shard_map/while/body/eval_jaxpr/bqhgd,bkhd->bhgqk/dot_general | solution.py:68
  3425.1 60.9 %fusion.424 = f32[16,16,256]{2,1,0:T(8,128)S(1)} fusion(f32[16,16,767,256]{3,2,1,0:T(8,128)} %get-tuple-element.605, f32[16,16,256]{2,1,0:T(8,128)S(1)} %get-tuple-element.606, pred[256,767]{0,1:T(8,128)(4,1)S(1)} %fusion.422), kind=kLoop, calls=%fused_computation.57.clone.1 | loop fusion | flops 200998912 | bytes 201785088 | tf_op jit(solution)/shard_map/while/body/eval_jaxpr/reduce_sum | solution.py:71
  3486.0 78.7 %bitcast_dynamic-update-slice_fusion.10 = bf16[2,16,256,16,1,64]{2,5,3,1,4,0:T(8,128)(2,1)} fusion(bf16[2,16,256,16,1,64]{2,5,3,1,4,0:T(8,128)(2,1)} %get-tuple-element.709, s32[]{:T(128)} %get-tuple-element.708, f32[16,16,256]{2,1,0:T(8,128)S(1)} %fusion.424, f32[16,16,256]{2,1,0:T(8,128)S(1)} %get-tuple-element.606, ...), kind=kOutput, calls=%fused_computation.64.clone.1 | convolution fusion | flops 6689587200 | bytes 235602176 | tf_op jit(solution)/shard_map/while/body/eval_jaxpr/bhgqk,bkhd->bqhgd/dot_general | solution.py:72
  3656.3 78.5 %fusion.180 = bf16[16,512,4096]{2,1,0:T(8,128)(2,1)} fusion(bf16[16,512,1024]{2,1,0:T(8,128)(2,1)} %get-tuple-element.400, f32[1024]{0:T(1024)S(1)} %bitcast.517, f32[16,512]{1,0:T(8,128)S(1)} %add_rsqrt_fusion.2, bf16[4,1024,4096]{2,1,0:T(8,128)(2,1)} %param.28), kind=kOutput, calls=%fused_computation.238 | convolution fusion | flops 68753031168 | bytes 92311552 | tf_op jit(solution)/shard_map/dot_general | solution.py:50
  3734.9 97.2 %fusion.171.clone.5 = bf16[16,512,4096]{2,1,0:T(8,128)(2,1)} fusion(bf16[16,512,4096]{2,1,0:T(8,128)(2,1)} %fusion.180, bf16[16,512,1024]{2,1,0:T(8,128)(2,1)} %get-tuple-element.400, f32[1024]{0:T(1024)S(1)} %bitcast.518, f32[16,512]{1,0:T(8,128)S(1)} %add_rsqrt_fusion.2, bf16[4,1024,4096]{2,1,0:T(8,128)(2,1)} %param.27), kind=kOutput, calls=%fused_computation.125.clone.clone.clone.clone.clone.clone.2 | convolution fusion | flops 69055021056 | bytes 159420416 | tf_op jit(solution)/shard_map/dot_general | solution.py:49
  3832.0 79.7 %fusion.144 = (f32[16,512]{1,0:T(8,128)S(1)}, bf16[16,512,1024]{2,1,0:T(8,128)(2,1)}) fusion(bf16[4,4096,1024]{2,1,0:T(8,128)(2,1)} %param.29, bf16[16,512,1024]{2,1,0:T(8,128)(2,1)} %get-tuple-element.400, bf16[16,512,4096]{2,1,0:T(8,128)(2,1)} %fusion.171.clone.5), kind=kOutput, calls=%fused_computation.180 | convolution fusion | flops 68769800192 | bytes 109084672 | tf_op jit(solution)/shard_map/dot_general | solution.py:52
  4098.7 100.8 %collective-permute-done.7 = bf16[16,511,16,64]{1,3,2,0:T(8,128)(2,1)} collective-permute-done((bf16[16,511,16,64]{1,3,2,0:T(8,128)(2,1)}, bf16[16,511,16,64]{1,3,2,0:T(8,128)(2,1)}, u32[]{:S(2)}, u32[]{:S(2)}) %collective-permute-start.7) | collective-permute-done | bytes 16744480 | tf_op jit(solution)/shard_map/ppermute | solution.py:90
  4223.2 156.0 %collective-permute-done.6 = bf16[16,511,16,64]{1,3,2,0:T(8,128)(2,1)} collective-permute-done((bf16[16,511,16,64]{1,3,2,0:T(8,128)(2,1)}, bf16[16,511,16,64]{1,3,2,0:T(8,128)(2,1)}, u32[]{:S(2)}, u32[]{:S(2)}) %collective-permute-start.6) | collective-permute-done | bytes 16744480 | tf_op jit(solution)/shard_map/ppermute | solution.py:90
  4408.9 455.3 %while.47 = (s32[]{:T(128)}, bf16[2,16,256,16,1,64]{2,5,3,1,4,0:T(8,128)(2,1)}, s32[2]{0:T(128)}, bf16[16,1023,16,64]{1,3,2,0:T(8,128)(2,1)}, s32[]{:T(128)}, /*...) while((s32[]{:T(128)}, ...), condition=%wide.region_22.23_spmd.clone, body=%wide.region_19.22_spmd.clone.sunk | while | flops 13476167680 | bytes 672663808 | solution.py:74
  4411.7 85.6 %fusion.428 = (f32[16,16,256]{2,1,0:T(8,128)S(1)}, f32[16,16,767,256]{3,2,1,0:T(8,128)}) fusion(pred[256,767]{0,1:T(8,128)(4,1)S(1)} %fusion.427, bf16[16,512,16,1,64]{1,4,2,0,3:T(8,128)(2,1)} %get-tuple-element.766, s32[]{:T(128)S(6)} %select_n.142, bf16[16,1023,16,64]{1,3,2,0:T(8,128)(2,1)} %get-tuple-element.765, s32[]{:T(128)S(6)} %select_n.143), kind=kOutput, calls=%fused_computation.81.clone.1 | convolution fusion | flops 6584795136 | bytes 235077376 | tf_op jit(solution)/shard_map/while/body/eval_jaxpr/bqhgd,bkhd->bhgqk/dot_general | solution.py:68
  4497.3 60.9 %fusion.429 = f32[16,16,256]{2,1,0:T(8,128)S(1)} fusion(f32[16,16,767,256]{3,2,1,0:T(8,128)} %get-tuple-element.615, f32[16,16,256]{2,1,0:T(8,128)S(1)} %get-tuple-element.616, pred[256,767]{0,1:T(8,128)(4,1)S(1)} %fusion.427), kind=kLoop, calls=%fused_computation.80.clone.1 | loop fusion | flops 200998912 | bytes 201785088 | tf_op jit(solution)/shard_map/while/body/eval_jaxpr/reduce_sum | solution.py:71
  4558.2 79.6 %bitcast_dynamic-update-slice_fusion.11 = bf16[2,16,256,16,1,64]{2,5,3,1,4,0:T(8,128)(2,1)} fusion(bf16[2,16,256,16,1,64]{2,5,3,1,4,0:T(8,128)(2,1)} %get-tuple-element.748, s32[]{:T(128)} %get-tuple-element.747, f32[16,16,256]{2,1,0:T(8,128)S(1)} %fusion.429, f32[16,16,256]{2,1,0:T(8,128)S(1)} %get-tuple-element.616, ...), kind=kOutput, calls=%fused_computation.87.clone.1 | convolution fusion | flops 6689587200 | bytes 235602176 | tf_op jit(solution)/shard_map/while/body/eval_jaxpr/bhgqk,bkhd->bqhgd/dot_general | solution.py:72
  4640.6 84.0 %fusion.428 = (f32[16,16,256]{2,1,0:T(8,128)S(1)}, f32[16,16,767,256]{3,2,1,0:T(8,128)}) fusion(pred[256,767]{0,1:T(8,128)(4,1)S(1)} %fusion.427, bf16[16,512,16,1,64]{1,4,2,0,3:T(8,128)(2,1)} %get-tuple-element.766, s32[]{:T(128)S(6)} %select_n.142, bf16[16,1023,16,64]{1,3,2,0:T(8,128)(2,1)} %get-tuple-element.765, s32[]{:T(128)S(6)} %select_n.143), kind=kOutput, calls=%fused_computation.81.clone.1 | convolution fusion | flops 6584795136 | bytes 235077376 | tf_op jit(solution)/shard_map/while/body/eval_jaxpr/bqhgd,bkhd->bhgqk/dot_general | solution.py:68
  4724.6 60.9 %fusion.429 = f32[16,16,256]{2,1,0:T(8,128)S(1)} fusion(f32[16,16,767,256]{3,2,1,0:T(8,128)} %get-tuple-element.615, f32[16,16,256]{2,1,0:T(8,128)S(1)} %get-tuple-element.616, pred[256,767]{0,1:T(8,128)(4,1)S(1)} %fusion.427), kind=kLoop, calls=%fused_computation.80.clone.1 | loop fusion | flops 200998912 | bytes 201785088 | tf_op jit(solution)/shard_map/while/body/eval_jaxpr/reduce_sum | solution.py:71
  4785.5 78.7 %bitcast_dynamic-update-slice_fusion.11 = bf16[2,16,256,16,1,64]{2,5,3,1,4,0:T(8,128)(2,1)} fusion(bf16[2,16,256,16,1,64]{2,5,3,1,4,0:T(8,128)(2,1)} %get-tuple-element.748, s32[]{:T(128)} %get-tuple-element.747, f32[16,16,256]{2,1,0:T(8,128)S(1)} %fusion.429, f32[16,16,256]{2,1,0:T(8,128)S(1)} %get-tuple-element.616, ...), kind=kOutput, calls=%fused_computation.87.clone.1 | convolution fusion | flops 6689587200 | bytes 235602176 | tf_op jit(solution)/shard_map/while/body/eval_jaxpr/bhgqk,bkhd->bqhgd/dot_general | solution.py:72
  4955.8 78.5 %fusion.176 = bf16[16,512,4096]{2,1,0:T(8,128)(2,1)} fusion(bf16[16,512,1024]{2,1,0:T(8,128)(2,1)} %get-tuple-element.404, f32[1024]{0:T(1024)S(1)} %bitcast.512, f32[16,512]{1,0:T(8,128)S(1)} %add_rsqrt_fusion, bf16[4,1024,4096]{2,1,0:T(8,128)(2,1)} %param.28), kind=kOutput, calls=%fused_computation.236 | convolution fusion | flops 68753031168 | bytes 92311552 | tf_op jit(solution)/shard_map/dot_general | solution.py:50
  5034.4 97.0 %fusion.388 = bf16[16,512,4096]{2,1,0:T(8,128)(2,1)} fusion(bf16[16,512,4096]{2,1,0:T(8,128)(2,1)} %fusion.176, bf16[16,512,1024]{2,1,0:T(8,128)(2,1)} %get-tuple-element.404, f32[1024]{0:T(1024)S(1)} %bitcast.513, f32[16,512]{1,0:T(8,128)S(1)} %add_rsqrt_fusion, bf16[4,1024,4096]{2,1,0:T(8,128)(2,1)} %param.27), kind=kOutput, calls=%fused_computation.124.clone.clone.clone.clone.2 | convolution fusion | flops 69055021056 | bytes 159420416 | tf_op jit(solution)/shard_map/dot_general | solution.py:49
  5131.4 78.6 %fusion.151 = bf16[16,512,1024]{2,1,0:T(8,128)(2,1)} fusion(bf16[16,512,1024]{2,1,0:T(8,128)(2,1)} %get-tuple-element.404, bf16[4,4096,1024]{2,1,0:T(8,128)(2,1)} %param.29, bf16[16,512,4096]{2,1,0:T(8,128)(2,1)} %fusion.388), kind=kOutput, calls=%fused_computation.187 | convolution fusion | flops 68744642560 | bytes 109051904 | tf_op jit(solution)/shard_map/dot_general | solution.py:52
  (171 shorter events, 1366.9 us)
Async XLA Ops:
  1.5 33.2 slice-start
  9.0 25.6 slice-start.1
  9.0 25.6 slice-start.2
  9.0 25.6 slice-start.3
  34.7 23.4 copy-start.15
  61.7 35.5 copy-start
  61.8 35.5 copy-start.4
  97.3 22.7 slice-start.4
  97.3 22.7 slice-start.5
  115.5 184.7 %collective-permute-start.1 = (bf16[16,511,16,64]{1,3,2,0:T(8,128)(2,1)}, bf16[16,511,16,64]{1,3,2,0:T(8,128)(2,1)}, u32[]{:S(2)}, u32[]{:S(2)}) collective-permute-start(bf16[16,511,16,64]{1,3,2,0:T(8,128)(2,1)} %pad_maximum_fusion.7), channel_id=1, source_target_pairs={{0,1},{1,2},{2,3},{4,5},{5,6},{6,7}} | collective-permute-start | bytes 50233352 | tf_op jit(solution)/shard_map/ppermute | solution.py:90
  147.0 41.6 copy-start.16
  186.1 293.9 %collective-permute-start = (bf16[16,511,16,64]{1,3,2,0:T(8,128)(2,1)}, bf16[16,511,16,64]{1,3,2,0:T(8,128)(2,1)}, u32[]{:S(2)}, u32[]{:S(2)}) collective-permute-start(bf16[16,511,16,64]{1,3,2,0:T(8,128)(2,1)} %slice.240), channel_id=1, source_target_pairs={{0,1},{1,2},{2,3},{4,5},{5,6},{6,7}} | collective-permute-start | bytes 50233352 | tf_op jit(solution)/shard_map/ppermute | solution.py:90
  965.2 58.1 %copy-start.14 = (bf16[1,16,64,1024]{3,2,1,0:T(8,128)(2,1)S(1)}, bf16[1,16,64,1024]{3,2,1,0:T(8,128)(2,1)}, u32[]{:S(2)}) copy-start(bf16[1,16,64,1024]{3,2,1,0:T(8,128)(2,1)} %get-tuple-element.367) | copy-start | bytes 6291460
  1023.4 33.5 copy-start.23
  1232.6 79.7 %copy-start.22 = (f32[1,1024]{1,0:T(1,128)S(1)}, f32[1,1024]{1,0:T(1,128)}, u32[]{:S(2)}) copy-start(f32[1,1024]{1,0:T(1,128)} %get-tuple-element.388) | copy-start | bytes 12292
  1337.7 25.8 copy-start.1
  1337.7 25.8 copy-start.5
  1398.3 21.5 copy-start.13
  1415.4 184.6 %collective-permute-start.3 = (bf16[16,511,16,64]{1,3,2,0:T(8,128)(2,1)}, bf16[16,511,16,64]{1,3,2,0:T(8,128)(2,1)}, u32[]{:S(2)}, u32[]{:S(2)}) collective-permute-start(bf16[16,511,16,64]{1,3,2,0:T(8,128)(2,1)} %pad_maximum_fusion.6), channel_id=1, source_target_pairs={{0,1},{1,2},{2,3},{4,5},{5,6},{6,7}} | collective-permute-start | bytes 50233352 | tf_op jit(solution)/shard_map/ppermute | solution.py:90
  1483.5 296.3 %collective-permute-start.2 = (bf16[16,511,16,64]{1,3,2,0:T(8,128)(2,1)}, bf16[16,511,16,64]{1,3,2,0:T(8,128)(2,1)}, u32[]{:S(2)}, u32[]{:S(2)}) collective-permute-start(bf16[16,511,16,64]{1,3,2,0:T(8,128)(2,1)} %slice.245), channel_id=1, source_target_pairs={{0,1},{1,2},{2,3},{4,5},{5,6},{6,7}} | collective-permute-start | bytes 50233352 | tf_op jit(solution)/shard_map/ppermute | solution.py:90
  2265.1 58.1 %copy-start.12 = (bf16[1,16,64,1024]{3,2,1,0:T(8,128)(2,1)S(1)}, bf16[1,16,64,1024]{3,2,1,0:T(8,128)(2,1)}, u32[]{:S(2)}) copy-start(bf16[1,16,64,1024]{3,2,1,0:T(8,128)(2,1)} %get-tuple-element.366) | copy-start | bytes 6291460
  2323.2 33.5 copy-start.21
  2532.4 79.7 %copy-start.20 = (f32[1,1024]{1,0:T(1,128)S(1)}, f32[1,1024]{1,0:T(1,128)}, u32[]{:S(2)}) copy-start(f32[1,1024]{1,0:T(1,128)} %get-tuple-element.390) | copy-start | bytes 12292
  2637.5 25.8 copy-start.2
  2637.5 25.8 copy-start.6
  2698.1 21.5 copy-start.11
  2715.2 184.6 %collective-permute-start.5 = (bf16[16,511,16,64]{1,3,2,0:T(8,128)(2,1)}, bf16[16,511,16,64]{1,3,2,0:T(8,128)(2,1)}, u32[]{:S(2)}, u32[]{:S(2)}) collective-permute-start(bf16[16,511,16,64]{1,3,2,0:T(8,128)(2,1)} %pad_maximum_fusion.5), channel_id=1, source_target_pairs={{0,1},{1,2},{2,3},{4,5},{5,6},{6,7}} | collective-permute-start | bytes 50233352 | tf_op jit(solution)/shard_map/ppermute | solution.py:90
  2783.3 296.3 %collective-permute-start.4 = (bf16[16,511,16,64]{1,3,2,0:T(8,128)(2,1)}, bf16[16,511,16,64]{1,3,2,0:T(8,128)(2,1)}, u32[]{:S(2)}, u32[]{:S(2)}) collective-permute-start(bf16[16,511,16,64]{1,3,2,0:T(8,128)(2,1)} %slice.250), channel_id=1, source_target_pairs={{0,1},{1,2},{2,3},{4,5},{5,6},{6,7}} | collective-permute-start | bytes 50233352 | tf_op jit(solution)/shard_map/ppermute | solution.py:90
  3564.7 58.1 %copy-start.10 = (bf16[1,16,64,1024]{3,2,1,0:T(8,128)(2,1)S(1)}, bf16[1,16,64,1024]{3,2,1,0:T(8,128)(2,1)}, u32[]{:S(2)}) copy-start(bf16[1,16,64,1024]{3,2,1,0:T(8,128)(2,1)} %get-tuple-element.368) | copy-start | bytes 6291460
  3622.8 33.5 copy-start.19
  3832.0 79.7 %copy-start.18 = (f32[1,1024]{1,0:T(1,128)S(1)}, f32[1,1024]{1,0:T(1,128)}, u32[]{:S(2)}) copy-start(f32[1,1024]{1,0:T(1,128)} %get-tuple-element.387) | copy-start | bytes 12292
  3937.1 25.8 copy-start.3
  3937.2 25.8 copy-start.7
  3997.7 21.5 copy-start.9
  4014.8 184.6 %collective-permute-start.7 = (bf16[16,511,16,64]{1,3,2,0:T(8,128)(2,1)}, bf16[16,511,16,64]{1,3,2,0:T(8,128)(2,1)}, u32[]{:S(2)}, u32[]{:S(2)}) collective-permute-start(bf16[16,511,16,64]{1,3,2,0:T(8,128)(2,1)} %pad_maximum_fusion.4), channel_id=1, source_target_pairs={{0,1},{1,2},{2,3},{4,5},{5,6},{6,7}} | collective-permute-start | bytes 50233352 | tf_op jit(solution)/shard_map/ppermute | solution.py:90
  4082.9 296.3 %collective-permute-start.6 = (bf16[16,511,16,64]{1,3,2,0:T(8,128)(2,1)}, bf16[16,511,16,64]{1,3,2,0:T(8,128)(2,1)}, u32[]{:S(2)}, u32[]{:S(2)}) collective-permute-start(bf16[16,511,16,64]{1,3,2,0:T(8,128)(2,1)} %slice.255), channel_id=1, source_target_pairs={{0,1},{1,2},{2,3},{4,5},{5,6},{6,7}} | collective-permute-start | bytes 50233352 | tf_op jit(solution)/shard_map/ppermute | solution.py:90
  4864.2 58.1 %copy-start.8 = (bf16[1,16,64,1024]{3,2,1,0:T(8,128)(2,1)S(1)}, bf16[1,16,64,1024]{3,2,1,0:T(8,128)(2,1)}, u32[]{:S(2)}) copy-start(bf16[1,16,64,1024]{3,2,1,0:T(8,128)(2,1)} %get-tuple-element.365) | copy-start | bytes 6291460
  4922.3 33.5 copy-start.17
where the time goes:
time: 5230 us; the launch traced here: 5210 us
  matrix products  2770 us (53%)
  waiting for transfers between devices  1020 us (20%)
  other arithmetic  958 us (18%)
  local copies, waits for them, and re-layouts  436 us (8%)
    ppermute x8, waiting for transfers between devices, local_stack(): lax.ppermute((key_r[:, tokens - halo:], value_r[:, tokens - halo:]), 'sp'...  1020 us
    dot_general x8, matrix products, one_block(): jnp.einsum('bqhgd,bkhd->bhgqk', query_blk, key_blk, preferred_element_typ...  678 us
    dot_general x8, matrix products, one_block(): jnp.einsum('bhgqk,bkhd->bqhgd', probabilities, value_blk, preferred_eleme...  633 us
    reduce_sum x8, other arithmetic, one_block(): probabilities = jax.nn.softmax(scores, axis=-1).astype(jnp.bfloat16)  488 us
    dot_general x4, matrix products, feed_forward(): jnp.dot(normed, w_gate, preferred_element_type=jnp.float32)  388 us
    dot_general x4, matrix products, feed_forward(): jnp.dot(hidden_act, w_down, preferred_element_type=jnp.float32)  318 us
    dot_general x4, matrix products, feed_forward(): jnp.dot(normed, w_up, preferred_element_type=jnp.float32)  314 us
    concatenate x12, other arithmetic, rotate(): jnp.concatenate([first * cos_a - second * sin_a, second * cos_a + first *...  265 us
  transfers between devices with their start and end apart: 8, of which 8 were waited for; matrix products, arithmetic and copies ran while one was open for 8% of the time, Pallas kernels for 0%

commit v1 on v0

v1 whole, which is shorter than its diff:
```python
import functools
import math
import jax
import jax.numpy as jnp
from jax import lax
from jax.experimental import pallas as pl
from jax.experimental.pallas import tpu as pltpu
from jax.sharding import PartitionSpec as P

EPS = 1e-5
ROPE_THETA = 10000.0
WINDOW = 512
HEADS = 16
HEAD_DIM = 64
HALF = HEAD_DIM // 2
QB = 256
TM = 512
FC = 1024
F32 = jnp.float32
BF16 = jnp.bfloat16
NT = (((1,), (1,)), ((), ()))
NEG = -1e30
EXP2_SCALE = math.log2(math.e) / math.sqrt(HEAD_DIM)
VMEM_LIMIT = 64 * 1024 * 1024 - 65536


def rms_norm(x_f32, gain):
    inv_rms = lax.rsqrt(jnp.mean(x_f32 * x_f32, axis=-1, keepdims=True) + EPS)
    return (x_f32 * inv_rms * gain).astype(BF16)


def resident(shape, index):
    return pl.BlockSpec(shape, index, pipeline_mode=pl.Buffered(1))


def qkv_kernel(x_ref, g_ref, cos_t_ref, sin_t_ref, cos_ref, sin_ref, wq_ref, wk_ref, wv_ref, q_ref, k_ref, v_ref):
    h = rms_norm(x_ref[...].astype(F32), g_ref[...])
    cos_t, sin_t = cos_t_ref[...], sin_t_ref[...]
    for g in range(HEADS // 4):
        r0 = 4 * HEAD_DIM * g
        rows = slice(r0, r0 + 4 * HEAD_DIM)
        q = lax.dot_general(wq_ref[rows, :], h, NT, preferred_element_type=F32)
        for j in range(4):
            a, b = q[HEAD_DIM * j:HEAD_DIM * j + HALF], q[HEAD_DIM * j + HALF:HEAD_DIM * (j + 1)]
            q_ref[r0 + HEAD_DIM * j:r0 + HEAD_DIM * j + HALF, :] = (a * cos_t - b * sin_t).astype(BF16)
            q_ref[r0 + HEAD_DIM * j + HALF:r0 + HEAD_DIM * (j + 1), :] = (b * cos_t + a * sin_t).astype(BF16)
        wk = jnp.concatenate(
            [wk_ref[r0 + HEAD_DIM * j + HALF * p:r0 + HEAD_DIM * j + HALF * (p + 1), :] for p in range(2) for j in range(4)], axis=0)
        k = lax.dot_general(h, wk, NT, preferred_element_type=F32)
        a, b = k[:, :128], k[:, 128:]
        cos, sin = cos_ref[...], sin_ref[...]
        k_ref[:, r0:r0 + 128] = (a * cos - b * sin).astype(BF16)
        k_ref[:, r0 + 128:r0 + 256] = (b * cos + a * sin).astype(BF16)
        v_ref[rows, :] = lax.dot_general(wv_ref[rows, :], h, NT, preferred_element_type=F32).astype(BF16)


def qkv_call(layer, x, gain, tables, wq, wk, wv):
    tokens, dim = x.shape
    weight = resident((None, dim, dim), lambda i: (layer, 0, 0))
    return pl.pallas_call(
        qkv_kernel,
        out_shape=(jax.ShapeDtypeStruct((dim, tokens), BF16), jax.ShapeDtypeStruct((tokens, dim), BF16),
                   jax.ShapeDtypeStruct((dim, tokens), BF16)),
        grid=(tokens // TM,),
        in_specs=[pl.BlockSpec((TM, dim), lambda i: (i, 0)),
                  pl.BlockSpec((None, 1, dim), lambda i: (layer, 0, 0)),
                  pl.BlockSpec((HALF, TM), lambda i: (0, i)), pl.BlockSpec((HALF, TM), lambda i: (0, i)),
                  pl.BlockSpec((TM, 128), lambda i: (i, 0)), pl.BlockSpec((TM, 128), lambda i: (i, 0)),
                  weight, weight, weight],
        out_specs=(pl.BlockSpec((dim, TM), lambda i: (0, i)), pl.BlockSpec((TM, dim), lambda i: (i, 0)),
                   pl.BlockSpec((dim, TM), lambda i: (0, i))),
        compiler_params=pltpu.CompilerParams(vmem_limit_bytes=VMEM_LIMIT),
        name="qkv",
    )(x, gain, *tables, wq, wk, wv)


def attend_head(head, blk, n_blocks, tri, q_ref, k_ref, v_ref, ot_ref):
    g, j = divmod(head, 4)
    r0 = head * HEAD_DIM
    parts = []
    for piece in (q_ref[r0:r0 + HALF, :], q_ref[r0 + HALF:r0 + HEAD_DIM, :]):
        parts += [piece if n == j else jnp.zeros((HALF, QB), BF16) for n in range(4)]
    rhs = jnp.concatenate(parts, axis=0)

    def scores(back):
        start = pl.multiple_of((blk - back) * QB, QB)
        return jnp.dot(k_ref[pl.ds(start, QB), 256 * g:256 * g + 256], rhs, preferred_element_type=F32)

    def values(back):
        start = pl.multiple_of((blk - back) * QB, QB)
        return v_ref[r0:r0 + HEAD_DIM, pl.ds(start, QB)]

    own = scores(0)
    far = scores(2) if n_blocks == 3 else None
    mid = scores(1) if n_blocks >= 2 else None
    p_own = [[None, None], [None, None]]
    p_far = [[None, None], [None, None]]
    p_mid, sums = [], []
    for c in range(2):
        cols = slice(128 * c, 128 * c + 128)
        tiles = []
        for a in range(2):
            rows = slice(128 * a, 128 * a + 128)
            if a == c:
                tiles.append(jnp.where(tri, own[rows, cols], far[rows, cols] if far is not None else NEG))
            elif a < c:
                tiles.append(own[rows, cols])
            else:
                tiles.append(far[rows, cols] if far is not None else None)
        if mid is not None:
            tiles.append(mid[:, cols])
        top = functools.reduce(jnp.maximum, [jnp.max(t, axis=0, keepdims=True) for t in tiles if t is not None])
        total = 0.0
        for a, t in enumerate(tiles):
            if t is None:
                continue
            p = jnp.exp2((t - top) * EXP2_SCALE)
            total = total + jnp.sum(p, axis=0, keepdims=True)
            if a == 2:
                p_mid.append(p.astype(BF16))
            elif a == c:
                p_own[a][c] = jnp.where(tri, p, 0.0).astype(BF16)
                p_far[a][c] = jnp.where(tri, 0.0, p).astype(BF16)
            elif a < c:
                p_own[a][c] = p.astype(BF16)
            else:
                p_far[a][c] = p.astype(BF16)
        sums.append(total)
    zero = jnp.zeros((128, 128), BF16)

    def tile(p):
        return jnp.concatenate([jnp.concatenate([zero if t is None else t for t in row], axis=1) for row in p], axis=0)

    out = jnp.dot(values(0), tile(p_own), preferred_element_type=F32)
    if mid is not None:
        out = out + jnp.dot(values(1), jnp.concatenate(p_mid, axis=1), preferred_element_type=F32)
    if far is not None:
        out = out + jnp.dot(values(2), tile(p_far), preferred_element_type=F32)
    ot_ref[r0:r0 + HEAD_DIM, :] = (out * (1.0 / jnp.concatenate(sums, axis=1))).astype(BF16)


def attention_kernel(x_ref, q_ref, k_ref, v_ref, wo_ref, o_ref, ot_ref):
    blk = pl.program_id(1)
    tri = lax.broadcasted_iota(jnp.int32, (128, 128), 0) <= lax.broadcasted_iota(jnp.int32, (128, 128), 1)

    def run(n_blocks):
        for head in range(HEADS):
            attend_head(head, blk, n_blocks, tri, q_ref, k_ref, v_ref, ot_ref)

    pl.when(blk == 0)(lambda: run(1))
    pl.when(blk == 1)(lambda: run(2))
    pl.when(blk >= 2)(lambda: run(3))
    y = jnp.dot(jnp.transpose(ot_ref[...]), wo_ref[...], preferred_element_type=F32)
    o_ref[...] = (x_ref[...].astype(F32) + y).astype(BF16)


def attention_call(layer, seq, x, q, k, v, wo):
    tokens, dim = x.shape
    n = seq // QB
    return pl.pallas_call(
        attention_kernel,
        out_shape=jax.ShapeDtypeStruct((tokens, dim), BF16),
        grid=(tokens // seq, n),
        in_specs=[pl.BlockSpec((QB, dim), lambda b, i: (b * n + i, 0)),
                  pl.BlockSpec((dim, QB), lambda b, i: (0, b * n + i)),
                  pl.BlockSpec((seq, dim), lambda b, i: (b, 0)),
                  pl.BlockSpec((dim, seq), lambda b, i: (0, b)),
                  resident((None, dim, dim), lambda b, i: (layer, 0, 0))],
        out_specs=pl.BlockSpec((QB, dim), lambda b, i: (b * n + i, 0)),
        scratch_shapes=[pltpu.VMEM((dim, QB), BF16)],
        compiler_params=pltpu.CompilerParams(vmem_limit_bytes=VMEM_LIMIT),
        name="attention",
    )(x, q, k, v, wo)


def mlp_kernel(x_ref, g_ref, wg_ref, wu_ref, wd_ref, o_ref, act_ref):
    h = rms_norm(x_ref[...].astype(F32), g_ref[...])
    for c in range(wg_ref.shape[1] // FC):
        cols = slice(c * FC, (c + 1) * FC)
        a = jnp.dot(h, wg_ref[:, cols], preferred_element_type=F32).astype(BF16).astype(F32)
        b = jnp.dot(h, wu_ref[:, cols], preferred_element_type=F32).astype(BF16).astype(F32)
        act_ref[:, cols] = (a * (1.0 / (1.0 + jnp.exp(-a))) * b).astype(BF16)
    y = jnp.dot(act_ref[...], wd_ref[...], preferred_element_type=F32)
    o_ref[...] = (x_ref[...].astype(F32) + y).astype(BF16)


def mlp_call(layer, x, gain, wg, wu, wd):
    tokens, dim = x.shape
    ff = wg.shape[2]
    return pl.pallas_call(
        mlp_kernel,
        out_shape=jax.ShapeDtypeStruct((tokens, dim), BF16),
        grid=(tokens // TM,),
        in_specs=[pl.BlockSpec((TM, dim), lambda i: (i, 0)),
                  pl.BlockSpec((None, 1, dim), lambda i: (layer, 0, 0)),
                  resident((None, dim, ff), lambda i: (layer, 0, 0)),
                  resident((None, dim, ff), lambda i: (layer, 0, 0)),
                  resident((None, ff, dim), lambda i: (layer, 0, 0))],
        out_specs=pl.BlockSpec((TM, dim), lambda i: (i, 0)),
        scratch_shapes=[pltpu.VMEM((TM, ff), BF16)],
        compiler_params=pltpu.CompilerParams(vmem_limit_bytes=VMEM_LIMIT),
        name="mlp",
    )(x, gain, wg, wu, wd)


def rope_tables(positions):
    inv_freq = ROPE_THETA ** (-2.0 * jnp.arange(HALF, dtype=F32) / HEAD_DIM)
    angle = positions.astype(F32)[:, None] * inv_freq
    cos, sin = jnp.cos(angle), jnp.sin(angle)
    return cos.T, sin.T, jnp.tile(cos, (1, 4)), jnp.tile(sin, (1, 4))


def solution(mesh):
    def local_stack(hidden, positions, norm_attn, norm_mlp, w_query, w_key, w_value, w_out, w_gate, w_up, w_down):
        layers, dim = norm_attn.shape
        x = lax.all_to_all(hidden, 'sp', split_axis=0, concat_axis=1, tiled=True)
        pos = lax.all_to_all(positions, 'sp', split_axis=0, concat_axis=1, tiled=True)
        n_seq, seq = pos.shape
        x = x.reshape(n_seq * seq, dim)
        tables = rope_tables(pos.reshape(-1))
        out_in = [jnp.transpose(w, (0, 2, 3, 1)).reshape(layers, dim, dim) for w in (w_query, w_key, w_value)]
        wo = w_out.reshape(layers, dim, dim)
        g1, g2 = norm_attn.reshape(layers, 1, dim), norm_mlp.reshape(layers, 1, dim)
        for layer in range(layers):
            q, k, v = qkv_call(layer, x, g1, tables, *out_in)
            x = attention_call(layer, seq, x, q, k, v, wo)
            x = mlp_call(layer, x, g2, w_gate, w_up, w_down)
        return lax.all_to_all(x.reshape(n_seq, seq, dim), 'sp', split_axis=1, concat_axis=0, tiled=True)

    row_spec = P('dp', 'sp', None)
    return jax.shard_map(local_stack, mesh=mesh,
                         in_specs=(row_spec, P('dp', 'sp'), P(), P(), P(), P(), P(), P(), P(), P(), P()),
                         out_specs=row_spec, check_vma=False)
```

time: 5230 us -> 2520 us (0.48)
  matrix products: 2770 us -> 0 us
  Pallas kernels: 0 us -> 2080 us
  other arithmetic: 958 us -> 8.47 us
  waiting for transfers between devices: 1020 us -> 156 us
  local copies, waits for them, and re-layouts: 436 us -> 63.2 us
  blocking collectives: 0 us -> 193 us
    dot_general x44 -> x0, matrix products: 2770 us -> none  [the longest x8 678 us: one_block(): jnp.einsum('bqhgd,bkhd->bhgqk', query_blk, key_blk, preferred_element_typ...]
    pallas_call x0 -> x12, Pallas kernels: none -> 2080 us  [the longest x4 914 us: mlp_call(): pl.pallas_call(mlp_kernel, out_shape=jax.ShapeDtypeStruct((tokens, dim),...]
    ppermute x8 -> x0, waiting for transfers between devices: 1020 us -> none  [local_stack(): lax.ppermute((key_r[:, tokens - halo:], value_r[:, tokens - halo:]), 'sp'...]
    reduce_sum x9 -> x0, other arithmetic: 495 us -> none  [the longest x8 488 us: one_block(): probabilities = jax.nn.softmax(scores, axis=-1).astype(jnp.bfloat16)]
    concatenate x20 -> x0, other arithmetic: 452 us -> none  [the longest x12 265 us: rotate(): jnp.concatenate([first * cos_a - second * sin_a, second * cos_a + first *...]
    all_to_all x0 -> x2, blocking collectives: none -> 193 us  [the longest x1 186 us: local_stack(): lax.all_to_all(x.reshape(n_seq, seq, dim), 'sp', split_axis=1, concat_axi...]
    all_to_all x0 -> x1, waiting for transfers between devices: none -> 156 us  [local_stack(): x = lax.all_to_all(hidden, 'sp', split_axis=0, concat_axis=1, tiled=True)]
    transpose x4 -> x0, local copies, waits for them, and re-layouts: 125 us -> none  [window_attention(): return jnp.moveaxis(blocks, 0, 1).reshape(batch, tokens, -1)]
  transfers between devices with their start and end apart: 8 -> 1, of which waited for: 8 -> 1; matrix products, arithmetic and copies ran while one was open for 8% -> 1% of each run, Pallas kernels for 0% -> 0%
where the time goes in v1:
time: 2520 us; the launch traced here: 2500 us
  Pallas kernels  2080 us (83%)
  blocking collectives  193 us (8%)
  waiting for transfers between devices  156 us (6%)
  local copies, waits for them, and re-layouts  63.2 us (3%)
    pallas_call x4, Pallas kernels, mlp_call(): pl.pallas_call(mlp_kernel, out_shape=jax.ShapeDtypeStruct((tokens, dim),...  914 us
    pallas_call x4, Pallas kernels, attention_call(): pl.pallas_call(attention_kernel, out_shape=jax.ShapeDtypeStruct((tokens,...  901 us
    pallas_call x4, Pallas kernels, qkv_call(): pl.pallas_call(qkv_kernel, out_shape=(jax.ShapeDtypeStruct((dim, tokens),...  260 us
    all_to_all x1, blocking collectives, local_stack(): lax.all_to_all(x.reshape(n_seq, seq, dim), 'sp', split_axis=1, concat_axi...  186 us
    all_to_all x1, waiting for transfers between devices, local_stack(): x = lax.all_to_all(hidden, 'sp', split_axis=0, concat_axis=1, tiled=True)  156 us
  transfers between devices with their start and end apart: 1, of which 1 were waited for; matrix products, arithmetic and copies ran while one was open for 1% of the time, Pallas kernels for 0%

profile of v1, /device:TPU:1, one launch (start us, length us, event | category | flops | bytes accessed | tf_op | source)
XLA Modules:
  0.0 2504.6 jit_solution(2573201716880375727)
XLA Ops:
  0.0 0.8 all_to_all.37
  0.8 7.2 all_to_all.46
  8.0 0.0 copy-start
  8.0 0.0 copy-start.1
  8.0 7.8 all-to-all-start
  15.9 0.0 copy-done
  15.9 0.6 reshape.101.g_ref
  16.5 0.0 copy-done.1
  16.5 0.6 reshape.106.g_ref
  17.1 3.7 multiply_sine_fusion
  20.8 2.4 tile.20
  23.3 5.6 copy.28.sin_ref
  28.9 2.4 tile.8
  31.3 5.6 copy.27.cos_ref
  36.9 4.8 multiply_sine_fusion.1
  41.6 156.1 %all-to-all-done = bf16[16,512,1024]{2,1,0:T(8,128)(2,1)} async-done(((bf16[16,512,1024]{2,1,0:T(8,128)(2,1)}), bf16[16,512,1024]{2,1,0:T(8,128)(2,1)}, u32[]{:S(2)}, u32[]{:S(2)}) %all-to-all-start) | async-done | bytes 16777248 | tf_op jit(solution)/shard_map/all_to_all | solution.py:216
  197.8 13.9 copy.25
  211.7 65.1 %qkv.4 = (bf16[1024,8192]{1,0:T(8,128)(2,1)}, bf16[8192,1024]{1,0:T(8,128)(2,1)}, bf16[1024,8192]{1,0:T(8,128)(2,1)}) custom-call(bf16[8192,1024]{1,0:T(8,128)(2,1)} %bitcast.27, f32[4,1,1024]{2,1,0:T(1,128)} %reshape.101.g_ref, f32[32,8192]{1,0:T(8,128)} %get-tuple-element.32.cos_t_ref, f32[32,8192]{1,0:T(8,128)} %get-tuple-element.31.sin_t_ref, ...), custom_call_target="tpu_custom_call" | custom-call | tf_op jit(solution)/shard_map/qkv/pallas_call | solution.py:60
  276.8 225.4 %attention.4.x_ref = bf16[8192,1024]{1,0:T(8,128)(2,1)} custom-call(bf16[8192,1024]{1,0:T(8,128)(2,1)} %bitcast.28, bf16[1024,8192]{1,0:T(8,128)(2,1)} %get-tuple-element.17.q_ref, bf16[8192,1024]{1,0:T(8,128)(2,1)} %get-tuple-element.18.k_ref, bf16[1024,8192]{1,0:T(8,128)(2,1)} %get-tuple-element.19.v_ref, bf16[4,1024,1024]{2,1,0:T(8,128)(2,1)} %bitcast.41), custom_call_target="tpu_custom_call" | custom-call | tf_op jit(solution)/shard_map/attention/pallas_call | solution.py:160
  502.2 228.6 %mlp.4.x_ref = bf16[8192,1024]{1,0:T(8,128)(2,1)} custom-call(bf16[8192,1024]{1,0:T(8,128)(2,1)} %attention.4.x_ref, f32[4,1,1024]{2,1,0:T(1,128)} %reshape.106.g_ref, bf16[4,1024,4096]{2,1,0:T(8,128)(2,1)} %wg_ref.7, bf16[4,1024,4096]{2,1,0:T(8,128)(2,1)} %wu_ref.7, bf16[4,4096,1024]{2,1,0:T(8,128)(2,1)} %wd_ref.7), custom_call_target="tpu_custom_call" | custom-call | tf_op jit(solution)/shard_map/mlp/pallas_call | solution.py:190
  730.7 65.1 %qkv.5 = (bf16[1024,8192]{1,0:T(8,128)(2,1)}, bf16[8192,1024]{1,0:T(8,128)(2,1)}, bf16[1024,8192]{1,0:T(8,128)(2,1)}) custom-call(bf16[8192,1024]{1,0:T(8,128)(2,1)} %mlp.4.x_ref, f32[4,1,1024]{2,1,0:T(1,128)} %reshape.101.g_ref, f32[32,8192]{1,0:T(8,128)} %get-tuple-element.32.cos_t_ref, f32[32,8192]{1,0:T(8,128)} %get-tuple-element.31.sin_t_ref, ...), custom_call_target="tpu_custom_call" | custom-call | tf_op jit(solution)/shard_map/qkv/pallas_call | solution.py:60
  795.9 225.3 %attention.5.x_ref = bf16[8192,1024]{1,0:T(8,128)(2,1)} custom-call(bf16[8192,1024]{1,0:T(8,128)(2,1)} %mlp.4.x_ref, bf16[1024,8192]{1,0:T(8,128)(2,1)} %get-tuple-element.20.q_ref, bf16[8192,1024]{1,0:T(8,128)(2,1)} %get-tuple-element.21.k_ref, bf16[1024,8192]{1,0:T(8,128)(2,1)} %get-tuple-element.22.v_ref, bf16[4,1024,1024]{2,1,0:T(8,128)(2,1)} %bitcast.42), custom_call_target="tpu_custom_call" | custom-call | tf_op jit(solution)/shard_map/attention/pallas_call | solution.py:160
  1021.1 228.5 %mlp.5.x_ref = bf16[8192,1024]{1,0:T(8,128)(2,1)} custom-call(bf16[8192,1024]{1,0:T(8,128)(2,1)} %attention.5.x_ref, f32[4,1,1024]{2,1,0:T(1,128)} %reshape.106.g_ref, bf16[4,1024,4096]{2,1,0:T(8,128)(2,1)} %wg_ref.7, bf16[4,1024,4096]{2,1,0:T(8,128)(2,1)} %wu_ref.7, bf16[4,4096,1024]{2,1,0:T(8,128)(2,1)} %wd_ref.7), custom_call_target="tpu_custom_call" | custom-call | tf_op jit(solution)/shard_map/mlp/pallas_call | solution.py:190
  1249.6 65.1 %qkv.6 = (bf16[1024,8192]{1,0:T(8,128)(2,1)}, bf16[8192,1024]{1,0:T(8,128)(2,1)}, bf16[1024,8192]{1,0:T(8,128)(2,1)}) custom-call(bf16[8192,1024]{1,0:T(8,128)(2,1)} %mlp.5.x_ref, f32[4,1,1024]{2,1,0:T(1,128)} %reshape.101.g_ref, f32[32,8192]{1,0:T(8,128)} %get-tuple-element.32.cos_t_ref, f32[32,8192]{1,0:T(8,128)} %get-tuple-element.31.sin_t_ref, ...), custom_call_target="tpu_custom_call" | custom-call | tf_op jit(solution)/shard_map/qkv/pallas_call | solution.py:60
  1314.7 225.3 %attention.6.x_ref = bf16[8192,1024]{1,0:T(8,128)(2,1)} custom-call(bf16[8192,1024]{1,0:T(8,128)(2,1)} %mlp.5.x_ref, bf16[1024,8192]{1,0:T(8,128)(2,1)} %get-tuple-element.23.q_ref, bf16[8192,1024]{1,0:T(8,128)(2,1)} %get-tuple-element.24.k_ref, bf16[1024,8192]{1,0:T(8,128)(2,1)} %get-tuple-element.25.v_ref, bf16[4,1024,1024]{2,1,0:T(8,128)(2,1)} %bitcast.43), custom_call_target="tpu_custom_call" | custom-call | tf_op jit(solution)/shard_map/attention/pallas_call | solution.py:160
  1540.0 228.5 %mlp.6.x_ref = bf16[8192,1024]{1,0:T(8,128)(2,1)} custom-call(bf16[8192,1024]{1,0:T(8,128)(2,1)} %attention.6.x_ref, f32[4,1,1024]{2,1,0:T(1,128)} %reshape.106.g_ref, bf16[4,1024,4096]{2,1,0:T(8,128)(2,1)} %wg_ref.7, bf16[4,1024,4096]{2,1,0:T(8,128)(2,1)} %wu_ref.7, bf16[4,4096,1024]{2,1,0:T(8,128)(2,1)} %wd_ref.7), custom_call_target="tpu_custom_call" | custom-call | tf_op jit(solution)/shard_map/mlp/pallas_call | solution.py:190
  1768.4 65.1 %qkv.7 = (bf16[1024,8192]{1,0:T(8,128)(2,1)}, bf16[8192,1024]{1,0:T(8,128)(2,1)}, bf16[1024,8192]{1,0:T(8,128)(2,1)}) custom-call(bf16[8192,1024]{1,0:T(8,128)(2,1)} %mlp.6.x_ref, f32[4,1,1024]{2,1,0:T(1,128)} %reshape.101.g_ref, f32[32,8192]{1,0:T(8,128)} %get-tuple-element.32.cos_t_ref, f32[32,8192]{1,0:T(8,128)} %get-tuple-element.31.sin_t_ref, ...), custom_call_target="tpu_custom_call" | custom-call | tf_op jit(solution)/shard_map/qkv/pallas_call | solution.py:60
  1833.5 225.1 %attention.7.x_ref = bf16[8192,1024]{1,0:T(8,128)(2,1)} custom-call(bf16[8192,1024]{1,0:T(8,128)(2,1)} %mlp.6.x_ref, bf16[1024,8192]{1,0:T(8,128)(2,1)} %get-tuple-element.26.q_ref, bf16[8192,1024]{1,0:T(8,128)(2,1)} %get-tuple-element.27.k_ref, bf16[1024,8192]{1,0:T(8,128)(2,1)} %get-tuple-element.28.v_ref, bf16[4,1024,1024]{2,1,0:T(8,128)(2,1)} %bitcast.44), custom_call_target="tpu_custom_call" | custom-call | tf_op jit(solution)/shard_map/attention/pallas_call | solution.py:160
  2058.6 228.4 %mlp.7 = bf16[8192,1024]{1,0:T(8,128)(2,1)} custom-call(bf16[8192,1024]{1,0:T(8,128)(2,1)} %attention.7.x_ref, f32[4,1,1024]{2,1,0:T(1,128)} %reshape.106.g_ref, bf16[4,1024,4096]{2,1,0:T(8,128)(2,1)} %wg_ref.7, bf16[4,1024,4096]{2,1,0:T(8,128)(2,1)} %wu_ref.7, bf16[4,4096,1024]{2,1,0:T(8,128)(2,1)} %wd_ref.7), custom_call_target="tpu_custom_call" | custom-call | tf_op jit(solution)/shard_map/mlp/pallas_call | solution.py:190
  2287.0 19.3 copy.35
  2306.3 185.9 %all_to_all.47 = bf16[4,2048,1024]{2,0,1:T(4,128)(2,1)S(1)} all-to-all(bf16[4,2048,1024]{2,0,1:T(4,128)(2,1)S(1)} %copy.35), channel_id=1, replica_groups=mesh['dp'=2,'sp'=4] {'sp'}, dimensions={1} | all-to-all | bytes 33554432 | tf_op jit(solution)/shard_map/all_to_all | solution.py:228
  2492.2 11.9 copy.36
  (4 shorter events, 0.0 us)
Async XLA Ops:
  8.0 7.9 copy-start
  8.0 8.5 copy-start.1
  8.0 189.7 %all-to-all-start = ((bf16[16,512,1024]{2,1,0:T(8,128)(2,1)}), bf16[16,512,1024]{2,1,0:T(8,128)(2,1)}, u32[]{:S(2)}, u32[]{:S(2)}) async-start(bf16[16,512,1024]{2,1,0:T(8,128)(2,1)} %param.11), calls=%async_computation | async-start | bytes 33554432 | tf_op jit(solution)/shard_map/all_to_all | solution.py:216
